TPU v7x, 32 devices: a whole 2x2x4 slice. The times are simulated.
32 devices in a mesh: seq: 4 (over y, x), wshard: 8 (over z, core).
Axes of the slice: x: 2, y: 2, z: 4, core: 2. Of those that a mesh axis runs over, the one named last changes fastest.
Arguments:
- layer_input: bfloat16 [8, 1024, 1536], P('wshard', 'seq'), may hold values from -6 to 6
- lengths: int32 [8], P('wshard'), may hold values from 256 to 1024, as said below
- norm_attn: float32 [1536], replicated, may hold values from 0.1 to 1.9
- w_query: bfloat16 [1536, 1536], P('wshard'), may hold values from -0.15625 to 0.15625
- w_key: bfloat16 [1536, 1536], P('wshard'), may hold values from -0.15625 to 0.15625
- w_value: bfloat16 [1536, 1536], P('wshard'), may hold values from -0.15625 to 0.15625
- w_ogate: bfloat16 [1536, 1536], P('wshard'), may hold values from -0.15625 to 0.15625
- w_forget: bfloat16 [1536, 24], P('wshard'), may hold values from -0.15625 to 0.15625
- forget_bias: float32 [24], replicated, may hold values from 3.5 to 8
- w_out: bfloat16 [1536, 1536], P('wshard'), may hold values from -1 to 1
- norm_ffn: float32 [1536], replicated, may hold values from 0.1 to 1.9
- w_gate: bfloat16 [1536, 4096], P('wshard'), may hold values from -0.15625 to 0.15625
- w_up: bfloat16 [1536, 4096], P('wshard'), may hold values from -0.15625 to 0.15625
- w_down: bfloat16 [4096, 1536], P('wshard'), may hold values from -0.09375 to 0.09375
- output_grad: bfloat16 [8, 1024, 1536], P('wshard', 'seq'), may hold values from -6 to 6
Outputs:
- layer_output: bfloat16 [8, 1024, 1536], P('wshard', 'seq')
- grad_input: float32 [8, 1024, 1536], P('wshard', 'seq')
- grad_norm_attn: float32 [1536], replicated
- grad_w_query: float32 [1536, 1536], P('wshard')
- grad_w_key: float32 [1536, 1536], P('wshard')
- grad_w_value: float32 [1536, 1536], P('wshard')
- grad_w_ogate: float32 [1536, 1536], P('wshard')
- grad_w_forget: float32 [1536, 24], P('wshard')
- grad_forget_bias: float32 [24], replicated
- grad_w_out: float32 [1536, 1536], P('wshard')
- grad_norm_ffn: float32 [1536], replicated
- grad_w_gate: float32 [1536, 4096], P('wshard')
- grad_w_up: float32 [1536, 4096], P('wshard')
- grad_w_down: float32 [4096, 1536], P('wshard')
Inputs may be any that keep to these rules, and one draw needn't show every extreme that they name: Each sequence has 1024 slots of which the first lengths[s] are valid; in every draw one sequence is full and one has exactly 256 valid slots.
All inputs are finite; a program needn't handle non-finite values.
Results may differ from a plain program's by a relative error of at most 0.014.
Values may be sent and summed in bfloat16 or wider, within the bound.
A program may use at most 320 MiB of HBM per device.

v0:
```python
import jax
import jax.numpy as jnp
from jax import lax
from jax.sharding import PartitionSpec as P

EPS = 1e-06
NEG_FILL = -1e30
BF16 = jnp.bfloat16
F32 = jnp.float32


def product(left, right):
    return jnp.dot(left, right, preferred_element_type=F32)


def product_tn(left, right):
    return lax.dot_general(left, right, (((0,), (0,)), ((), ())), preferred_element_type=F32)


def product_nt(left, right):
    return lax.dot_general(left, right, (((1,), (1,)), ((), ())), preferred_element_type=F32)


def rms_norm(values, gain):
    return values * lax.rsqrt(jnp.mean(values * values, axis=-1, keepdims=True) + EPS) * gain


def gate_product(attended, gate_pre):
    return attended * jax.nn.sigmoid(gate_pre)


def swiglu(gate, upward):
    return jax.nn.silu(gate) * upward


def gather_rows(shard):
    return lax.all_gather(shard, "wshard", axis=0, tiled=True)


def scatter_rows(partial):
    return lax.psum_scatter(partial.astype(BF16), "wshard", scatter_dimension=0, tiled=True)


def gather_slots(shard):
    return lax.all_gather(shard, "seq", axis=0, tiled=True)


def scatter_slots(partial):
    return lax.psum_scatter(partial.astype(BF16), "seq", scatter_dimension=0, tiled=True).astype(
        F32
    )


def share_columns(share):
    return lax.all_gather(share, "seq", axis=1, tiled=True).astype(F32)


def block_scores(query_block, key_block, cum_rows, cum_keys, first_row, length, scale):
    plain = jnp.einsum("qhd,khd->hqk", query_block, key_block, preferred_element_type=F32) * scale
    plain = plain + cum_rows.T[:, :, None] - cum_keys.T[:, None, :]
    rows = first_row + jnp.arange(query_block.shape[0], dtype=jnp.int32)
    columns = jnp.arange(key_block.shape[0], dtype=jnp.int32)
    allowed = (columns[None, :] <= rows[:, None]) & (columns[None, :] < length)
    return jnp.where(allowed[None], plain, NEG_FILL)


def attention_forward(query, key, value, cumulative, length, scale, block):
    slots = query.shape[0]
    blocks = []
    log_totals = []
    for first in range(0, slots, block):
        last = first + block
        masked = block_scores(
            query[first:last],
            key[:last],
            cumulative[first:last],
            cumulative[:last],
            first,
            length,
            scale,
        )
        log_total = jax.nn.logsumexp(masked, axis=-1, keepdims=True)
        probability = jnp.exp(masked - log_total).astype(BF16)
        blocks.append(
            jnp.einsum("hqk,khd->qhd", probability, value[:last], preferred_element_type=F32)
        )
        log_totals.append(log_total)
    return (jnp.concatenate(blocks, axis=0).astype(BF16), log_totals)


def attention_backward(query, key, value, grad, cumulative, log_totals, length, scale, block):
    slots, heads, size = query.shape
    grad_query = []
    grad_key = jnp.zeros((slots, heads, size), F32)
    grad_value = jnp.zeros((slots, heads, size), F32)
    grad_cum = jnp.zeros((slots, heads), F32)
    for number, first in enumerate(range(0, slots, block)):
        last = first + block
        masked = block_scores(
            query[first:last],
            key[:last],
            cumulative[first:last],
            cumulative[:last],
            first,
            length,
            scale,
        )
        probability = jnp.exp(masked - log_totals[number])
        probability_low = probability.astype(BF16)
        grad_block = grad[first:last]
        grad_probability = jnp.einsum(
            "qhd,khd->hqk", grad_block, value[:last], preferred_element_type=F32
        )
        row_dot = jnp.sum(grad_probability * probability, axis=-1, keepdims=True)
        score_terms = probability * (grad_probability - row_dot)
        grad_scores = score_terms.astype(BF16)
        grad_cum = grad_cum.at[first:last].add(jnp.sum(score_terms, axis=2).T)
        grad_cum = grad_cum.at[:last].add(-jnp.sum(score_terms, axis=1).T)
        grad_query.append(
            jnp.einsum("hqk,khd->qhd", grad_scores, key[:last], preferred_element_type=F32)
        )
        grad_key = grad_key.at[:last].add(
            jnp.einsum("hqk,qhd->khd", grad_scores, query[first:last], preferred_element_type=F32)
        )
        grad_value = grad_value.at[:last].add(
            jnp.einsum("hqk,qhd->khd", probability_low, grad_block, preferred_element_type=F32)
        )
    grad_query = (jnp.concatenate(grad_query, axis=0) * scale).astype(BF16)
    return (grad_query, (grad_key * scale).astype(BF16), grad_value.astype(BF16), grad_cum)


def on_device(
    layer_input,
    lengths,
    norm_attn,
    w_query,
    w_key,
    w_value,
    w_ogate,
    w_forget,
    forget_bias,
    w_out,
    norm_ffn,
    w_gate,
    w_up,
    w_down,
    output_grad,
):
    tokens, width = layer_input.shape[1:]
    heads = forget_bias.shape[0]
    groups = lax.axis_size("seq")
    owners = lax.axis_size("wshard")
    local_heads = heads // groups
    head_size = width // heads
    slots = tokens * groups
    part = width // groups
    units = w_gate.shape[1]
    own_units = units // owners
    piece = own_units // groups
    local_units = units // groups
    block = min(512, slots)
    scale = head_size ** (-0.5)
    length = lengths[0]
    rank = lax.axis_index("seq")
    positions = rank * tokens + jnp.arange(tokens, dtype=jnp.int32)
    valid_slots = (positions < length).astype(F32)[:, None]
    inputs = layer_input[0].astype(F32)
    cotangent = output_grad[0].astype(F32) * valid_slots

    def columns(weight):
        return lax.dynamic_slice_in_dim(weight, rank * part, part, 1)

    def unit_columns(weight):
        cut = lax.dynamic_index_in_dim(
            weight.reshape(-1, owners, groups, piece), rank, 2, keepdims=False
        )
        return cut.reshape(-1, local_units)

    pad = -local_heads % 128
    forget_columns = jnp.pad(
        lax.dynamic_slice_in_dim(w_forget, rank * local_heads, local_heads, 1), ((0, 0), (0, pad))
    )
    normed_attn = gather_slots(rms_norm(inputs, norm_attn).astype(BF16))
    full_attn = gather_rows(
        jnp.concatenate(
            [columns(w_query), columns(w_key), columns(w_value), columns(w_ogate), forget_columns],
            axis=1,
        )
    )
    cut_out = gather_rows(columns(w_out))
    full_out = lax.all_to_all(cut_out, "seq", split_axis=0, concat_axis=1, tiled=True)
    full_gate_up = gather_rows(jnp.concatenate([unit_columns(w_gate), unit_columns(w_up)], axis=1))
    full_down = gather_rows(lax.dynamic_slice_in_dim(w_down, rank * piece, piece, 0))
    cotangent_low = gather_slots(cotangent.astype(BF16))
    query = product(normed_attn, full_attn[:, :part]).astype(BF16)
    key = product(normed_attn, full_attn[:, part : 2 * part]).astype(BF16)
    value = product(normed_attn, full_attn[:, 2 * part : 3 * part]).astype(BF16)
    gate_pre = product(normed_attn, full_attn[:, 3 * part : 4 * part])
    forget_pre = product(normed_attn, full_attn[:, 4 * part :])[:, :local_heads].astype(BF16)
    query = query.reshape(slots, local_heads, head_size)
    key = key.reshape(slots, local_heads, head_size)
    value = value.reshape(slots, local_heads, head_size)
    bias_local = lax.dynamic_slice_in_dim(forget_bias, rank * local_heads, local_heads)
    forget_total = forget_pre.astype(F32) + bias_local
    log_forget, pull_forget = jax.vjp(jax.nn.log_sigmoid, forget_total)
    cumulative = jnp.cumsum(log_forget, axis=0)
    head_output, log_totals = attention_forward(query, key, value, cumulative, length, scale, block)
    attended = head_output.reshape(slots, part).astype(F32)
    gated_full, pull_gate = jax.vjp(gate_product, attended, gate_pre)
    gated = gated_full.astype(BF16)
    middle = inputs + scatter_slots(product(gated, full_out))
    normed_ffn_full, pull_ffn_norm = jax.vjp(rms_norm, middle, norm_ffn)
    normed_ffn = gather_slots(normed_ffn_full.astype(BF16))
    gate_value = product(normed_ffn, full_gate_up[:, :local_units])
    up_value = product(normed_ffn, full_gate_up[:, local_units:])
    hidden_full, pull_swiglu = jax.vjp(swiglu, gate_value, up_value)
    hidden = hidden_full.astype(BF16)
    result = middle + scatter_slots(product(hidden, full_down))
    layer_output = result.astype(BF16)[None]
    grad_hidden = product_nt(cotangent_low, full_down)
    grad_gate_full, grad_up_full = pull_swiglu(grad_hidden)
    grad_gate_up = jnp.concatenate([grad_gate_full.astype(BF16), grad_up_full.astype(BF16)], axis=1)
    grad_normed_ffn = scatter_slots(product_nt(grad_gate_up, full_gate_up))
    share_down = scatter_rows(product_tn(hidden, cotangent_low))
    share_gate_up = scatter_rows(product_tn(normed_ffn, grad_gate_up))
    grad_middle_part, grad_norm_ffn = pull_ffn_norm(grad_normed_ffn)
    grad_middle = cotangent + grad_middle_part
    grad_branch = gather_slots(grad_middle.astype(BF16))
    grad_gated = product_nt(grad_branch, full_out)
    grad_w_out = product_tn(gated, grad_branch).astype(BF16)
    share_out = scatter_rows(
        lax.all_to_all(grad_w_out, "seq", split_axis=1, concat_axis=0, tiled=True)
    )
    grad_attended_full, grad_gate_pre_full = pull_gate(grad_gated)
    grad_attended = grad_attended_full.astype(BF16).reshape(slots, local_heads, head_size)
    grad_gate_pre = grad_gate_pre_full.astype(BF16)
    grad_query, grad_key, grad_value, grad_cum = attention_backward(
        query, key, value, grad_attended, cumulative, log_totals, length, scale, block
    )
    grad_log_forget = jnp.flip(jnp.cumsum(jnp.flip(grad_cum, 0), axis=0), 0)
    grad_forget_total = pull_forget(grad_log_forget)[0]
    grad_bias_local = jnp.sum(grad_forget_total, axis=0)
    grad_bias = lax.dynamic_update_slice_in_dim(
        jnp.zeros((heads,), F32), grad_bias_local, rank * local_heads, 0
    )
    grad_attn = jnp.concatenate(
        [
            grad_query.reshape(slots, part),
            grad_key.reshape(slots, part),
            grad_value.reshape(slots, part),
            grad_gate_pre,
            jnp.pad(grad_forget_total.astype(BF16), ((0, 0), (0, pad))),
        ],
        axis=1,
    )
    grad_normed_attn = scatter_slots(product_nt(grad_attn, full_attn))
    share_attn = scatter_rows(product_tn(normed_attn, grad_attn))
    unused_normed, pull_attn_norm = jax.vjp(rms_norm, inputs, norm_attn)
    grad_input_part, grad_norm_attn = pull_attn_norm(grad_normed_attn)
    grad_input = (grad_middle + grad_input_part)[None]
    rows = w_query.shape[0]
    all_down = lax.all_gather(share_down, "seq", axis=0, tiled=True).astype(F32)
    all_gate_up = lax.all_gather(share_gate_up, "seq", axis=0, tiled=False)
    all_gate_up = all_gate_up.reshape(groups, rows, 2, owners, piece).transpose(2, 1, 3, 0, 4)
    all_gate_up = all_gate_up.reshape(2, rows, units).astype(F32)
    all_out = share_columns(share_out)
    all_attn = lax.all_gather(share_attn, "seq", axis=0, tiled=False)

    def whole(first, size):
        cut = all_attn[:, :, first : first + size].transpose(1, 0, 2)
        return cut.reshape(rows, groups * size).astype(F32)

    small = lax.psum((grad_norm_attn, grad_norm_ffn, grad_bias), ("seq", "wshard"))
    return (
        layer_output,
        grad_input,
        small[0],
        whole(0, part),
        whole(part, part),
        whole(2 * part, part),
        whole(3 * part, part),
        whole(4 * part, local_heads),
        small[2],
        all_out,
        small[1],
        all_gate_up[0],
        all_gate_up[1],
        all_down,
    )


def solution(mesh):
    rows = P("wshard", None)
    slots = P("wshard", "seq", None)
    return jax.shard_map(
        on_device,
        mesh=mesh,
        in_specs=(
            slots,
            P("wshard"),
            P(),
            rows,
            rows,
            rows,
            rows,
            rows,
            P(),
            rows,
            P(),
            rows,
            rows,
            rows,
            slots,
        ),
        out_specs=(
            slots,
            slots,
            P(),
            rows,
            rows,
            rows,
            rows,
            rows,
            P(),
            rows,
            P(),
            rows,
            rows,
            rows,
        ),
        check_vma=False,
    )
```

profile of v0, /device:TPU:0, one launch (start us, length us, event | category | flops | bytes accessed | tf_op | source)
XLA Modules:
  0.0 979.0 jit_solution(494081339802589565)
XLA Ops:
  19.4 16.4 %all-gather.18.cloned.1.call-done = bf16[1536,384]{1,0:T(8,128)(2,1)} async-done(((bf16[192,384]{1,0:T(8,128)(2,1)}), bf16[1536,384]{1,0:T(8,128)(2,1)}) %all-gather.18.cloned.1.call-update) | async-done | bytes 1179664 | tf_op jit(solution)/shard_map/all_gather | solution.py:37
  35.8 3.5 all-to-all-start
  41.4 21.1 %all-to-all-done = bf16[4,384,384]{2,1,0:T(8,128)(2,1)S(1)} async-done(((bf16[4,384,384]{2,1,0:T(8,128)(2,1)}), bf16[4,384,384]{2,1,0:T(8,128)(2,1)S(1)}, u32[]{:S(2)}, u32[]{:S(2)}) %all-to-all-start) | async-done | bytes 1179680 | tf_op jit(solution)/shard_map/all_to_all | solution.py:191
  64.0 23.1 %all-gather.14.cloned.1.call-done = bf16[1024,1536]{1,0:T(8,128)(2,1)} async-done(((bf16[256,1536]{1,0:T(8,128)(2,1)}), bf16[1024,1536]{1,0:T(8,128)(2,1)}) %all-gather.14.cloned.1.call-update) | async-done | bytes 3145744 | tf_op jit(solution)/shard_map/all_gather | solution.py:45
  87.0 57.1 %all-gather.16.cloned.1.call-done = bf16[1536,1664]{1,0:T(8,128)(2,1)} async-done(((bf16[192,1664]{1,0:T(8,128)(2,1)}), bf16[1536,1664]{1,0:T(8,128)(2,1)}) %all-gather.16.cloned.1.call-update) | async-done | bytes 5111824 | tf_op jit(solution)/shard_map/all_gather | solution.py:37
  144.2 3.1 fusion.64
  150.3 3.8 convolution_convert_fusion.8
  154.1 3.1 convolution_convert_fusion.10
  157.3 2.8 convolution_convert_fusion.9
  163.4 3.6 fusion.86
  167.0 2.8 exponential_reduce_fusion
  171.5 2.3 fusion.51
  173.9 3.1 add_divide_fusion.1
  178.1 3.5 convolution_convert_fusion.4
  184.8 4.1 reshape.507
  188.9 2.3 reshape.509
  191.2 6.7 dynamic-slice_reduce_fusion
  199.1 25.4 %reduce-scatter.9.cloned.1.call-done = bf16[256,1536]{1,0:T(8,128)(2,1)} async-done(((bf16[1024,1536]{1,0:T(8,128)(2,1)}), bf16[256,1536]{1,0:T(8,128)(2,1)}) %reduce-scatter.9.cloned.1.call-update) | async-done | bytes 786448 | tf_op jit(solution)/shard_map/reduce_scatter | solution.py:49
  228.6 42.0 %all-gather.26.cloned.1.call-done = bf16[1024,1536]{1,0:T(8,128)(2,1)} async-done(((bf16[256,1536]{1,0:T(8,128)(2,1)}), bf16[1024,1536]{1,0:T(8,128)(2,1)}) %all-gather.26.cloned.1.call-update) | async-done | bytes 3145744 | tf_op jit(solution)/shard_map/all_gather | solution.py:45
  270.7 40.3 %all-gather.24.cloned.1.call-done = bf16[1024,1536]{1,0:T(8,128)(2,1)} async-done(((bf16[128,1536]{1,0:T(8,128)(2,1)}), bf16[1024,1536]{1,0:T(8,128)(2,1)}) %all-gather.24.cloned.1.call-update) | async-done | bytes 3145744 | tf_op jit(solution)/shard_map/all_gather | solution.py:37
  311.0 8.2 fusion.88
  319.2 57.6 %all-gather.22.cloned.1.call-done = bf16[1536,2048]{1,0:T(8,128)(2,1)} async-done(((bf16[192,2048]{1,0:T(8,128)(2,1)}), bf16[1536,2048]{1,0:T(8,128)(2,1)}) %all-gather.22.cloned.1.call-update) | async-done | bytes 6291472 | tf_op jit(solution)/shard_map/all_gather | solution.py:37
  376.8 44.9 %all-gather.20.cloned.1.call-done = bf16[1024,1536]{1,0:T(8,128)(2,1)} async-done(((bf16[256,1536]{1,0:T(8,128)(2,1)}), bf16[1024,1536]{1,0:T(8,128)(2,1)}) %all-gather.20.cloned.1.call-update) | async-done | bytes 3145744 | tf_op jit(solution)/shard_map/all_gather | solution.py:45
  421.8 8.5 fusion.6
  430.3 8.5 fusion.4
  440.1 9.4 convolution_convert_fusion.2
  450.0 43.6 %reduce-scatter.13.cloned.1.call-done = bf16[256,1536]{1,0:T(8,128)(2,1)} async-done(((bf16[1024,1536]{1,0:T(8,128)(2,1)}), bf16[256,1536]{1,0:T(8,128)(2,1)}) %reduce-scatter.13.cloned.1.call-update) | async-done | bytes 786448 | tf_op jit(solution)/shard_map/reduce_scatter | solution.py:49
  493.6 2.4 fusion.28
  496.0 2.7 fusion.78
  498.8 7.6 convolution_convert_fusion.5
  506.5 11.6 %convolution_convert_fusion.1 = bf16[1536,2048]{1,0:T(8,128)(2,1)} fusion(bf16[1024,1536]{1,0:T(8,128)(2,1)} %all-gather.20.cloned.1.call-done, bf16[1024,1024]{0,1:T(8,128)(2,1)} %get-tuple-element.150, bf16[1024,1024]{0,1:T(8,128)(2,1)} %copy-done.58), kind=kOutput, calls=%fused_computation.7 | convolution fusion | flops 6453985280 | bytes 13631488 | tf_op jit(solution)/shard_map/dot_general | solution.py:17
  518.2 24.6 %all-gather.28.cloned.1.call-done = bf16[1024,1536]{1,0:T(8,128)(2,1)} async-done(((bf16[256,1536]{1,0:T(8,128)(2,1)}), bf16[1024,1536]{1,0:T(8,128)(2,1)}) %all-gather.28.cloned.1.call-update) | async-done | bytes 3145744 | tf_op jit(solution)/shard_map/all_gather | solution.py:45
  542.7 5.3 multiply_convert_fusion.2
  548.8 4.6 multiply_reduce_fusion.1
  553.4 5.2 fusion.80
  558.7 4.4 multiply_reduce_fusion
  563.1 5.7 fusion.79
  571.6 2.7 rev.8
  574.3 2.8 fusion.42
  577.2 5.3 fusion.12
  588.9 2.4 fusion.37
  594.7 7.9 convolution_convert_fusion
  603.3 3.8 convolution_convert_fusion.7
  607.3 18.7 %all_to_all.38 = bf16[384,4,384]{2,0,1:T(8,128)(2,1)} all-to-all(bf16[384,4,384]{2,0,1:T(8,128)(2,1)S(1)} %bitcast.215), channel_id=1, replica_groups=mesh['seq'=4,'wshard'=8] {'seq'}, dimensions={1} | all-to-all | bytes 2359296 | tf_op jit(solution)/shard_map/all_to_all | solution.py:232
  626.0 31.2 %reduce-scatter.21.cloned.1.call-done = bf16[192,2048]{1,0:T(8,128)(2,1)} async-done(((bf16[1536,2048]{1,0:T(8,128)(2,1)}), bf16[192,2048]{1,0:T(8,128)(2,1)}) %reduce-scatter.21.cloned.1.call-update) | async-done | bytes 786448 | tf_op jit(solution)/shard_map/reduce_scatter | solution.py:41
  657.3 10.2 %convolution_convert_fusion.3 = bf16[1024,1536]{1,0:T(8,128)(2,1)} fusion(bf16[1024,1664]{0,1:T(8,128)(2,1)} %copy-done.36, bf16[1536,1664]{1,0:T(8,128)(2,1)} %all-gather.16.cloned.1.call-done), kind=kOutput, calls=%fused_computation.25 | convolution fusion | flops 5236064256 | bytes 11665408 | tf_op jit(solution)/shard_map/dot_general | solution.py:21
  667.5 7.7 convolution_convert_fusion.6
  675.3 41.0 %reduce-scatter.17.cloned.1.call-done = bf16[192,1664]{1,0:T(8,128)(2,1)} async-done(((bf16[1536,1664]{1,0:T(8,128)(2,1)}), bf16[192,1664]{1,0:T(8,128)(2,1)}) %reduce-scatter.17.cloned.1.call-update) | async-done | bytes 638992 | tf_op jit(solution)/shard_map/reduce_scatter | solution.py:41
  716.3 31.0 %all-gather.30.cloned.1.call-done = bf16[512,1536]{1,0:T(8,128)(2,1)} async-done(((bf16[128,1536]{1,0:T(8,128)(2,1)}), bf16[512,1536]{1,0:T(8,128)(2,1)}) %all-gather.30.cloned.1.call-update) | async-done | bytes 1572880 | tf_op jit(solution)/shard_map/all_gather | solution.py:262
  747.4 3.5 convert_element_type.258
  750.9 31.5 %reduce-scatter.19.cloned.1.call-done = bf16[192,384]{1,0:T(8,128)(2,1)} async-done(((bf16[1536,384]{1,0:T(8,128)(2,1)}), bf16[192,384]{1,0:T(8,128)(2,1)}) %reduce-scatter.19.cloned.1.call-update) | async-done | bytes 147472 | tf_op jit(solution)/shard_map/reduce_scatter | solution.py:41
  782.5 14.6 %all_gather.52 = bf16[192,1536]{1,0:T(8,128)(2,1)S(1)} all-gather(bf16[192,384]{1,0:T(8,128)(2,1)} %reduce-scatter.19.cloned.1.call-done), channel_id=1, replica_groups=mesh['seq'=4,'wshard'=8] {'seq'}, dimensions={1}, use_global_device_ids=true | all-gather | bytes 737280 | tf_op jit(solution)/shard_map/all_gather | solution.py:55
  798.3 28.1 %all-gather.34.cloned.1.call-done = bf16[768,2048]{1,0:T(8,128)(2,1)} async-done(((bf16[192,2048]{1,0:T(8,128)(2,1)}), bf16[768,2048]{1,0:T(8,128)(2,1)}) %all-gather.34.cloned.1.call-update) | async-done | bytes 3145744 | tf_op jit(solution)/shard_map/all_gather | solution.py:263
  826.4 2.7 convert_bitcast_fusion
  832.7 3.8 copy.88
  836.4 5.0 squeeze.16
  841.5 5.7 copy.87
  847.2 5.3 squeeze.15
  852.5 20.6 %reduce-scatter.15.cloned.1.call-done = bf16[256,1536]{1,0:T(8,128)(2,1)} async-done(((bf16[1024,1536]{1,0:T(8,128)(2,1)}), bf16[256,1536]{1,0:T(8,128)(2,1)}) %reduce-scatter.15.cloned.1.call-update) | async-done | bytes 786448 | tf_op jit(solution)/shard_map/reduce_scatter | solution.py:49
  875.0 40.3 %all-reduce.5 = (f32[1536]{0:T(1024)}, f32[24]{0:T(128)}, f32[1536]{0:T(1024)}) all-reduce(f32[1536]{0:T(1024)S(1)} %get-tuple-element.140, f32[24]{0:T(128)S(1)} %negate_dynamic-update-slice_fusion, f32[1536]{0:T(1024)S(1)} %copy-done.41), channel_id=1, replica_groups=mesh['seq'=4,'wshard'=8] {'seq','wshard'}, use_global_device_ids=true, to_apply=%region_23.24 | all-reduce | flops 3096 | bytes 24768 | tf_op jit(solution)/shard_map/psum | solution.py:273
  915.4 5.4 reduce-scatter.11.cloned.1.call-done
  920.7 4.0 fusion.32
  924.7 36.9 %all-gather.32.cloned.1.call-done = bf16[768,1664]{1,0:T(8,128)(2,1)} async-done(((bf16[192,1664]{1,0:T(8,128)(2,1)}), bf16[768,1664]{1,0:T(8,128)(2,1)}) %all-gather.32.cloned.1.call-update) | async-done | bytes 2555920 | tf_op jit(solution)/shard_map/all_gather | solution.py:267
  962.5 3.5 convert_bitcast_fusion.1
  (265 shorter events, 61.9 us)
Async XLA Ops:
  7.2 176.7 %copy-start = (bf16[512,1536]{1,0:T(8,128)(2,1)S(1)}, bf16[512,1536]{1,0:T(8,128)(2,1)}, u32[]{:S(2)}) copy-start(bf16[512,1536]{1,0:T(8,128)(2,1)} %param.50) | copy-start | bytes 4718596
  7.2 28.6 %all-gather.18.cloned.1.call-start = ((), (), s32[]{:S(2)}) async-start(), calls=%async_computation.12 | async-start | bytes 1327104 | tf_op jit(solution)/shard_map/all_gather | solution.py:37
  9.0 78.1 %all-gather.14.cloned.1.call-start = ((), (), s32[]{:S(2)}) async-start(), calls=%async_computation.10 | async-start | bytes 3932160 | tf_op jit(solution)/shard_map/all_gather | solution.py:45
  11.5 28.5 %copy-start.56 = (f32[24]{0:T(128)S(1)}, f32[24]{0:T(128)}, u32[]{:S(2)}) copy-start(f32[24]{0:T(128)} %param.45) | copy-start | bytes 292
  13.8 130.4 %all-gather.16.cloned.1.call-start = ((), (), s32[]{:S(2)}) async-start(), calls=%async_computation.11 | async-start | bytes 5750784 | tf_op jit(solution)/shard_map/all_gather | solution.py:37
  35.8 26.8 %all-to-all-start = ((bf16[4,384,384]{2,1,0:T(8,128)(2,1)}), bf16[4,384,384]{2,1,0:T(8,128)(2,1)S(1)}, u32[]{:S(2)}, u32[]{:S(2)}) async-start(bf16[4,384,384]{2,1,0:T(8,128)(2,1)} %bitcast.248), calls=%async_computation | async-start | bytes 2359296 | tf_op jit(solution)/shard_map/all_to_all | solution.py:191
  39.3 185.2 %reduce-scatter.9.cloned.1.call-start = ((), (), s32[]{:S(2)}) async-start(), calls=%async_computation.13 | async-start | bytes 3932160 | tf_op jit(solution)/shard_map/reduce_scatter | solution.py:49
  40.1 107.2 %copy-start.52 = (f32[6]{0:T(128)}, f32[6]{0:T(128)S(1)}, u32[]{:S(2)}) copy-start(f32[6]{0:T(128)S(1)} %dynamic_slice.36) | copy-start | bytes 76
  150.3 3.9 copy-start.17
  154.1 8.9 copy-start.21
  154.1 6.1 copy-start.27
  157.3 12.6 %copy-start.15 = (bf16[512,384]{0,1:T(8,128)(2,1)}, bf16[512,384]{0,1:T(8,128)(2,1)S(1)}, u32[]{:S(2)}) copy-start(bf16[512,384]{0,1:T(8,128)(2,1)S(1)} %slice.294) | copy-start | bytes 1179652
  162.0 7.9 copy-start.3
  162.9 7.0 copy-start.32
  167.0 4.5 copy-start.2
  171.0 6.0 copy-start.22
  173.9 4.2 copy-start.14
  181.7 89.0 %all-gather.26.cloned.1.call-start = ((), (), s32[]{:S(2)}) async-start(), calls=%async_computation.18 | async-start | bytes 3932160 | tf_op jit(solution)/shard_map/all_gather | solution.py:45
  182.8 313.2 %copy-start.46 = (f32[256]{0:T(256)}, f32[256]{0:T(256)S(1)}, u32[]{:S(2)}) copy-start(f32[256]{0:T(256)S(1)} %compare_convert_fusion) | copy-start | bytes 3076
  183.9 127.1 %all-gather.24.cloned.1.call-start = ((), (), s32[]{:S(2)}) async-start(), calls=%async_computation.16 | async-start | bytes 3538944 | tf_op jit(solution)/shard_map/all_gather | solution.py:37
  184.7 4.2 copy-start.24
  184.7 192.1 %all-gather.22.cloned.1.call-start = ((), (), s32[]{:S(2)}) async-start(), calls=%async_computation.15 | async-start | bytes 7077888 | tf_op jit(solution)/shard_map/all_gather | solution.py:37
  191.2 33.3 %copy-start.4 = (bf16[1,256,1536]{2,1,0:T(8,128)(2,1)S(1)}, bf16[1,256,1536]{2,1,0:T(8,128)(2,1)}, u32[]{:S(2)}) copy-start(bf16[1,256,1536]{2,1,0:T(8,128)(2,1)} %param.37) | copy-start | bytes 2359300
  197.9 28.1 %copy-start.37 = (f32[1536]{0:T(1024)S(1)}, f32[1536]{0:T(1024)}, u32[]{:S(2)}) copy-start(f32[1536]{0:T(1024)} %param.47) | copy-start | bytes 18436
  199.0 222.7 %all-gather.20.cloned.1.call-start = ((), (), s32[]{:S(2)}) async-start(), calls=%async_computation.14 | async-start | bytes 3932160 | tf_op jit(solution)/shard_map/all_gather | solution.py:45
  226.0 270.0 %copy-start.42 = (f32[256]{0:T(256)}, f32[256]{0:T(256)S(1)}, u32[]{:S(2)}) copy-start(f32[256]{0:T(256)S(1)} %fusion.73) | copy-start | bytes 3076
  228.4 265.2 %reduce-scatter.13.cloned.1.call-start = ((), (), s32[]{:S(2)}) async-start(), calls=%async_computation.19 | async-start | bytes 3932160 | tf_op jit(solution)/shard_map/reduce_scatter | solution.py:49
  421.8 8.5 copy-start.54
  421.8 8.5 copy-start.55
  421.8 8.5 copy-start.57
  449.5 44.1 %copy-start.6 = (bf16[256,1536]{1,0:T(8,128)(2,1)S(1)}, bf16[256,1536]{1,0:T(8,128)(2,1)}, u32[]{:S(2)}) copy-start(bf16[256,1536]{1,0:T(8,128)(2,1)} %reduce-scatter.9.cloned.1.call-done) | copy-start | bytes 2359300
  449.5 93.2 %all-gather.28.cloned.1.call-start = ((), (), s32[]{:S(2)}) async-start(), calls=%async_computation.20 | async-start | bytes 3932160 | tf_op jit(solution)/shard_map/all_gather | solution.py:45
  496.0 10.4 %copy-start.50 = (f32[256]{0:T(256)}, f32[256]{0:T(256)S(1)}, u32[]{:S(2)}) copy-start(f32[256]{0:T(256)S(1)} %multiply_multiply_fusion.1) | copy-start | bytes 3076
  498.7 104.0 %reduce-scatter.23.cloned.1.call-start = ((), (), s32[]{:S(2)}) async-start(), calls=%async_computation.25 | async-start | bytes 3538944 | tf_op jit(solution)/shard_map/reduce_scatter | solution.py:41
  506.4 150.8 %reduce-scatter.21.cloned.1.call-start = ((), (), s32[]{:S(2)}) async-start(), calls=%async_computation.24 | async-start | bytes 7077888 | tf_op jit(solution)/shard_map/reduce_scatter | solution.py:41
  518.1 198.2 %reduce-scatter.17.cloned.1.call-start = ((), (), s32[]{:S(2)}) async-start(), calls=%async_computation.22 | async-start | bytes 5750784 | tf_op jit(solution)/shard_map/reduce_scatter | solution.py:41
  548.8 4.6 copy-start.33
  548.8 9.8 %slice-start = ((s8[12582912]{0:T(1024)(128)(4,1)}), s8[4194304]{0:T(1024)(128)(4,1)S(1)}, s32[]{:S(2)}) async-start(s8[12582912]{0:T(1024)(128)(4,1)} %bitcast.202), calls=%async_computation.29 | async-start | bytes 8388608
  548.8 9.8 %slice-start.1 = ((s8[12582912]{0:T(1024)(128)(4,1)}), s8[4194304]{0:T(1024)(128)(4,1)S(1)}, s32[]{:S(2)}) async-start(s8[12582912]{0:T(1024)(128)(4,1)} %bitcast.202), calls=%async_computation.30 | async-start | bytes 8388608
  553.4 5.2 slice-start.2
  574.3 9.5 slice-start.8
  577.2 5.5 copy-start.5
  577.2 5.5 copy-start.26
  577.2 6.6 slice-start.9
  577.2 8.0 slice-start.6
  582.5 4.8 slice-start.3
  583.8 3.8 slice-start.4
  585.1 3.7 slice-start.5
  602.7 144.7 %all-gather.30.cloned.1.call-start = ((), (), s32[]{:S(2)}) async-start(), calls=%async_computation.26 | async-start | bytes 1966080 | tf_op jit(solution)/shard_map/all_gather | solution.py:262
  603.3 179.2 %reduce-scatter.19.cloned.1.call-start = ((), (), s32[]{:S(2)}) async-start(), calls=%async_computation.23 | async-start | bytes 1327104 | tf_op jit(solution)/shard_map/reduce_scatter | solution.py:41
  626.0 200.4 %all-gather.34.cloned.1.call-start = ((), (), s32[]{:S(2)}) async-start(), calls=%async_computation.28 | async-start | bytes 3932160 | tf_op jit(solution)/shard_map/all_gather | solution.py:263
  657.3 215.9 %reduce-scatter.15.cloned.1.call-start = ((), (), s32[]{:S(2)}) async-start(), calls=%async_computation.21 | async-start | bytes 3932160 | tf_op jit(solution)/shard_map/reduce_scatter | solution.py:49
  667.5 253.2 %reduce-scatter.11.cloned.1.call-start = ((), (), s32[]{:S(2)}) async-start(), calls=%async_computation.17 | async-start | bytes 3932160 | tf_op jit(solution)/shard_map/reduce_scatter | solution.py:49
  675.3 286.3 %all-gather.32.cloned.1.call-start = ((), (), s32[]{:S(2)}) async-start(), calls=%async_computation.27 | async-start | bytes 3194880 | tf_op jit(solution)/shard_map/all_gather | solution.py:267
  847.2 26.0 %copy-start.40 = (f32[1536]{0:T(1024)S(1)}, f32[1536]{0:T(1024)}, u32[]{:S(2)}) copy-start(f32[1536]{0:T(1024)} %param.39) | copy-start | bytes 18436
  847.2 26.0 %copy-start.45 = (f32[256]{0:T(256)S(1)}, f32[256]{0:T(256)}, u32[]{:S(2)}) copy-start(f32[256]{0:T(256)} %copy-done.44) | copy-start | bytes 3076
  847.2 27.8 %copy-start.41 = (f32[1536]{0:T(1024)S(1)}, f32[1536]{0:T(1024)}, u32[]{:S(2)}) copy-start(f32[1536]{0:T(1024)} %get-tuple-element.138) | copy-start | bytes 18436
  847.2 68.2 %copy-start.49 = (f32[256]{0:T(256)S(1)}, f32[256]{0:T(256)}, u32[]{:S(2)}) copy-start(f32[256]{0:T(256)} %copy-done.48) | copy-start | bytes 3076
  847.2 73.5 %copy-start.8 = (bf16[256,1536]{1,0:T(8,128)(2,1)S(1)}, bf16[256,1536]{1,0:T(8,128)(2,1)}, u32[]{:S(2)}) copy-start(bf16[256,1536]{1,0:T(8,128)(2,1)} %reduce-scatter.13.cloned.1.call-done) | copy-start | bytes 2359300
  847.2 73.5 %copy-start.38 = (f32[1536]{0:T(1024)S(1)}, f32[1536]{0:T(1024)}, u32[]{:S(2)}) copy-start(f32[1536]{0:T(1024)} %param.47) | copy-start | bytes 18436
  847.2 73.5 %copy-start.43 = (f32[256]{0:T(256)S(1)}, f32[256]{0:T(256)}, u32[]{:S(2)}) copy-start(f32[256]{0:T(256)} %copy-done.42) | copy-start | bytes 3076
  847.2 73.5 %copy-start.47 = (f32[256]{0:T(256)S(1)}, f32[256]{0:T(256)}, u32[]{:S(2)}) copy-start(f32[256]{0:T(256)} %copy-done.46) | copy-start | bytes 3076
  847.2 73.5 %copy-start.51 = (f32[256]{0:T(256)S(1)}, f32[256]{0:T(256)}, u32[]{:S(2)}) copy-start(f32[256]{0:T(256)} %copy-done.50) | copy-start | bytes 3076
  968.0 4.0 copy-start.1
  (25 other events, 54.5 us)
Sparse Core Ops, SparseCore 0:
  10.2 25.4 all-gather.17
  38.2 48.8 all-gather.13
  89.3 54.8 all-gather.15
  181.8 42.6 reduce-scatter.8
  226.8 43.8 all-gather.25
  272.7 38.2 all-gather.23
  313.2 63.5 all-gather.21
  379.2 42.4 all-gather.19
  449.6 43.8 reduce-scatter.12
  498.9 43.8 all-gather.27
  545.6 40.3 reduce-scatter.22
  588.2 69.0 reduce-scatter.20
  659.6 56.7 reduce-scatter.16
  718.0 29.3 all-gather.29
  749.5 32.9 reduce-scatter.18
  784.2 42.1 all-gather.33
  829.2 43.8 reduce-scatter.14
  876.0 44.6 reduce-scatter.10
  922.6 38.9 all-gather.31
where the time goes:
time: 989 us; the launch traced here: 979 us
  waiting for transfers between devices  623 us (63%)
  matrix products  140 us (14%)
  blocking collectives  73.7 us (7%)
  local copies, waits for them, and re-layouts  68.5 us (7%)
  other arithmetic  53.1 us (5%)
  between operations  16.2 us (2%)
    all_gather x4, waiting for transfers between devices, gather_rows(): return lax.all_gather(shard, 'wshard', axis=0, tiled=True)  171 us
    all_gather x4, waiting for transfers between devices, gather_slots(): return lax.all_gather(shard, 'seq', axis=0, tiled=True)  135 us
    reduce_scatter x4, waiting for transfers between devices, scatter_rows(): lax.psum_scatter(partial.astype(BF16), 'wshard', scatter_dimension=0, til...  104 us
    reduce_scatter x4, waiting for transfers between devices, scatter_slots(): lax.psum_scatter(partial.astype(BF16), 'seq', scatter_dimension=0, tiled=...  95.1 us
    dot_general x9, matrix products, product(): return jnp.dot(left, right, preferred_element_type=F32)  44.1 us
    psum x1, blocking collectives, on_device(): lax.psum((grad_norm_attn, grad_norm_ffn, grad_bias), ('seq', 'wshard'))  40.3 us
    all_gather x1, waiting for transfers between devices, on_device(): all_attn = lax.all_gather(share_attn, 'seq', axis=0, tiled=False)  36.9 us
    dot_general x4, matrix products, product_nt(): lax.dot_general(left, right, (((1,), (1,)), ((), ())), preferred_element_...  33.1 us
  transfers between devices with their start and end apart: 20, of which 19 were waited for; matrix products, arithmetic and copies ran while one was open for 18% of the time, Pallas kernels for 0%

commit v1 on v0

--- a/solution.py
+++ b/solution.py
@@ -9,6 +9,27 @@
 F32 = jnp.float32
 
 
+def gather_around(shard, axis, dim):
+    count, index, rows = (lax.axis_size(axis), lax.axis_index(axis), shard.shape[dim])
+    right = [(i, (i + 1) % count) for i in range(count)]
+    left = [(i, (i - 1) % count) for i in range(count)]
+    out = jnp.zeros((*shard.shape[:dim], count * rows, *shard.shape[dim + 1 :]), shard.dtype)
+    out = lax.dynamic_update_slice_in_dim(out, shard, index * rows, axis=dim)
+    from_left = from_right = shard
+    half = count // 2
+    for hop in range(1, half + 1):
+        from_left = lax.ppermute(from_left, axis, right)
+        out = lax.dynamic_update_slice_in_dim(
+            out, from_left, (index - hop) % count * rows, axis=dim
+        )
+        if hop < count - half:
+            from_right = lax.ppermute(from_right, axis, left)
+            out = lax.dynamic_update_slice_in_dim(
+                out, from_right, (index + hop) % count * rows, axis=dim
+            )
+    return out
+
+
 def product(left, right):
     return jnp.dot(left, right, preferred_element_type=F32)
 
@@ -34,7 +55,7 @@
 
 
 def gather_rows(shard):
-    return lax.all_gather(shard, "wshard", axis=0, tiled=True)
+    return gather_around(shard, "wshard", 0)
 
 
 def scatter_rows(partial):

time: 989 us -> 849 us (0.86)
  waiting for transfers between devices: 623 us -> 406 us
  local copies, waits for them, and re-layouts: 68.5 us -> 113 us
  starting transfers between devices: 4.93 us -> 46 us
    all_gather x4 -> x0, waiting for transfers between devices: 171 us -> none  [gather_rows(): return lax.all_gather(shard, 'wshard', axis=0, tiled=True)]
    all_gather x4, waiting for transfers between devices: 135 us -> 23.2 us  [gather_slots(): return lax.all_gather(shard, 'seq', axis=0, tiled=True)]
    ppermute x0 -> x28, waiting for transfers between devices: none -> 82.5 us  [the longest x16 43.9 us: gather_around(): from_left = lax.ppermute(from_left, axis, right)]
    ppermute x0 -> x28, starting transfers between devices: none -> 41.7 us  [the longest x12 40.9 us: gather_around(): from_right = lax.ppermute(from_right, axis, left)]
    dynamic_update_slice x0 -> x32, local copies, waits for them, and re-layouts: none -> 34.6 us  [the longest x16 16 us: gather_around(): lax.dynamic_update_slice_in_dim(out, from_left, (index - hop) % count * r...]
    all_to_all x1, waiting for transfers between devices: 21.1 us -> 0.01 us  [on_device(): lax.all_to_all(cut_out, 'seq', split_axis=0, concat_axis=1, tiled=True)]
    unnamed x153 -> x140, local copies, waits for them, and re-layouts: 17.9 us -> 22 us
  transfers between devices with their start and end apart: 20 -> 44, of which waited for: 19 -> 27; matrix products, arithmetic and copies ran while one was open for 18% -> 24% of each run, Pallas kernels for 0% -> 0%
where the time goes in v1:
time: 849 us; the launch traced here: 843 us
  waiting for transfers between devices  406 us (48%)
  matrix products  138 us (16%)
  local copies, waits for them, and re-layouts  113 us (13%)
  blocking collectives  73.4 us (9%)
  other arithmetic  50.8 us (6%)
  starting transfers between devices  46 us (5%)
  between operations  16 us (2%)
    reduce_scatter x4, waiting for transfers between devices, scatter_rows(): lax.psum_scatter(partial.astype(BF16), 'wshard', scatter_dimension=0, til...  108 us
    reduce_scatter x4, waiting for transfers between devices, scatter_slots(): lax.psum_scatter(partial.astype(BF16), 'seq', scatter_dimension=0, tiled=...  95.9 us
    ppermute x16, waiting for transfers between devices, gather_around(): from_left = lax.ppermute(from_left, axis, right)  43.9 us
    dot_general x9, matrix products, product(): return jnp.dot(left, right, preferred_element_type=F32)  41.8 us
    ppermute x12, starting transfers between devices, gather_around(): from_right = lax.ppermute(from_right, axis, left)  40.9 us
    psum x1, blocking collectives, on_device(): lax.psum((grad_norm_attn, grad_norm_ffn, grad_bias), ('seq', 'wshard'))  40.3 us
    ppermute x12, waiting for transfers between devices, gather_around(): from_right = lax.ppermute(from_right, axis, left)  38.5 us
    all_gather x1, waiting for transfers between devices, on_device(): all_attn = lax.all_gather(share_attn, 'seq', axis=0, tiled=False)  36.4 us
  transfers between devices with their start and end apart: 44, of which 27 were waited for; matrix products, arithmetic and copies ran while one was open for 24% of the time, Pallas kernels for 0%

profile of v1, /device:TPU:0, one launch (start us, length us, event | category | flops | bytes accessed | tf_op | source)
XLA Modules:
  0.0 843.2 jit_solution(4040942955284742579)
XLA Ops:
  16.0 4.6 collective-permute-start.1
  23.3 3.5 collective-permute-start.8
  32.7 6.8 collective-permute-done.7
  39.6 3.5 collective-permute-start.10
  47.5 3.6 collective-permute-start.12
  52.4 6.3 collective-permute-done.11
  59.4 3.5 collective-permute-start.3
  67.3 3.7 all-to-all-start
  72.9 3.5 collective-permute-done.3
  76.4 3.8 collective-permute-start.5
  81.1 6.9 collective-permute-done.4
  107.0 3.8 convolution_convert_fusion.8
  120.5 3.6 fusion.86
  135.3 3.5 convolution_convert_fusion.4
  143.7 3.9 reshape.509
  147.6 6.6 dynamic-slice_reduce_fusion
  154.4 26.8 %reduce-scatter.9.cloned.1.call-done = bf16[256,1536]{1,0:T(8,128)(2,1)} async-done(((bf16[1024,1536]{1,0:T(8,128)(2,1)}), bf16[256,1536]{1,0:T(8,128)(2,1)}) %reduce-scatter.9.cloned.1.call-update) | async-done | bytes 786448 | tf_op jit(solution)/shard_map/reduce_scatter | solution.py:70
  188.9 3.5 collective-permute-start.22
  192.5 3.5 broadcast_in_dim.54
  196.9 3.6 collective-permute-done.21
  200.5 3.5 collective-permute-start.24
  205.6 10.5 %collective-permute-done.15 = bf16[192,2048]{1,0:T(8,128)(2,1)} collective-permute-done((bf16[192,2048]{1,0:T(8,128)(2,1)S(1)}, bf16[192,2048]{1,0:T(8,128)(2,1)}, u32[]{:S(2)}, u32[]{:S(2)}) %collective-permute-start.15) | collective-permute-done | bytes 786464 | tf_op jit(solution)/shard_map/ppermute | solution.py:26
  216.1 3.8 collective-permute-start.17
  219.9 4.6 collective-permute-done.24
  224.5 3.7 collective-permute-start.26
  234.0 5.0 collective-permute-done.25
  239.8 10.0 %collective-permute-done.26 = bf16[128,1536]{1,0:T(8,128)(2,1)S(1)} collective-permute-done((bf16[128,1536]{1,0:T(8,128)(2,1)S(1)}, bf16[128,1536]{1,0:T(8,128)(2,1)S(1)}, u32[]{:S(2)}, u32[]{:S(2)}) %collective-permute-start.26) | collective-permute-done | bytes 393248 | tf_op jit(solution)/shard_map/ppermute | solution.py:26
  250.5 3.7 collective-permute-start.19
  255.8 4.4 collective-permute-done.27
  262.8 8.4 collective-permute-done.19
  274.9 8.3 fusion.88
  283.3 6.6 fusion.6
  289.9 8.7 %fusion.4 = (bf16[1024,1024]{0,1:T(8,128)(2,1)S(1)}, bf16[1024,1024]{0,1:T(8,128)(2,1)S(1)}, bf16[1024,1024]{0,1:T(8,128)(2,1)}) fusion(f32[1024,1024]{0,1:T(8,128)S(1)} %copy-done.46, f32[1024,1024]{0,1:T(8,128)S(1)} %fusion.6, bf16[1024,1536]{1,0:T(8,128)(2,1)S(1)} %copy-done.44, bf16[1536,2048]{1,0:T(8,128)(2,1)} %constant_dynamic-update-slice_fusion.10), kind=kOutput, calls=%fused_computation.18 | convolution fusion | flops 3238002688 | bytes 20971520 | tf_op jit(solution)/shard_map/dot_general | solution.py:34
  300.6 10.1 %convolution_convert_fusion.2 = bf16[1024,1536]{1,0:T(8,128)(2,1)} fusion(bf16[1536,2048]{1,0:T(8,128)(2,1)} %constant_dynamic-update-slice_fusion.10, bf16[1024,1024]{0,1:T(8,128)(2,1)S(1)} %get-tuple-element.154, bf16[1024,1024]{0,1:T(8,128)(2,1)S(1)} %get-tuple-element.153), kind=kOutput, calls=%fused_computation.24 | convolution fusion | flops 6452412416 | bytes 13631488 | tf_op jit(solution)/shard_map/dot_general | solution.py:42
  310.7 42.7 %reduce-scatter.13.cloned.1.call-done = bf16[256,1536]{1,0:T(8,128)(2,1)} async-done(((bf16[1024,1536]{1,0:T(8,128)(2,1)}), bf16[256,1536]{1,0:T(8,128)(2,1)}) %reduce-scatter.13.cloned.1.call-update) | async-done | bytes 786448 | tf_op jit(solution)/shard_map/reduce_scatter | solution.py:70
  358.1 7.6 convolution_convert_fusion.5
  367.4 11.4 %convolution_convert_fusion.1 = bf16[1536,2048]{1,0:T(8,128)(2,1)} fusion(bf16[1024,1536]{1,0:T(8,128)(2,1)} %all-gather.12.cloned.1.call-done, bf16[1024,1024]{0,1:T(8,128)(2,1)} %copy-done.50, bf16[1024,1024]{0,1:T(8,128)(2,1)S(1)} %copy-done.49), kind=kOutput, calls=%fused_computation.7 | convolution fusion | flops 6453985280 | bytes 13631488 | tf_op jit(solution)/shard_map/dot_general | solution.py:38
  378.8 23.2 %all-gather.16.cloned.1.call-done = bf16[1024,1536]{1,0:T(8,128)(2,1)} async-done(((bf16[256,1536]{1,0:T(8,128)(2,1)}), bf16[1024,1536]{1,0:T(8,128)(2,1)}) %all-gather.16.cloned.1.call-update) | async-done | bytes 3145744 | tf_op jit(solution)/shard_map/all_gather | solution.py:66
  402.0 5.4 multiply_convert_fusion.2
  408.2 5.2 multiply_reduce_fusion.1
  416.7 4.2 multiply_reduce_fusion
  421.0 5.4 fusion.79
  432.5 5.0 fusion.12
  449.7 8.1 convolution_convert_fusion
  458.8 3.4 convolution_convert_fusion.7
  462.3 18.5 %all_to_all.38 = bf16[384,4,384]{2,0,1:T(8,128)(2,1)} all-to-all(bf16[384,4,384]{2,0,1:T(8,128)(2,1)S(1)} %bitcast.215), channel_id=1, replica_groups=mesh['seq'=4,'wshard'=8] {'seq'}, dimensions={1} | all-to-all | bytes 2359296 | tf_op jit(solution)/shard_map/all_to_all | solution.py:253
  480.9 35.8 %reduce-scatter.21.cloned.1.call-done = bf16[192,2048]{1,0:T(8,128)(2,1)} async-done(((bf16[1536,2048]{1,0:T(8,128)(2,1)}), bf16[192,2048]{1,0:T(8,128)(2,1)}) %reduce-scatter.21.cloned.1.call-update) | async-done | bytes 786448 | tf_op jit(solution)/shard_map/reduce_scatter | solution.py:62
  516.7 10.1 %convolution_convert_fusion.3 = bf16[1024,1536]{1,0:T(8,128)(2,1)} fusion(bf16[1024,1664]{0,1:T(8,128)(2,1)} %copy-done.35, bf16[1536,1664]{1,0:T(8,128)(2,1)} %constant_dynamic-update-slice_fusion.26), kind=kOutput, calls=%fused_computation.25 | convolution fusion | flops 5236064256 | bytes 11665408 | tf_op jit(solution)/shard_map/dot_general | solution.py:42
  528.4 6.8 convolution_convert_fusion.6
  535.3 40.8 %reduce-scatter.17.cloned.1.call-done = bf16[192,1664]{1,0:T(8,128)(2,1)} async-done(((bf16[1536,1664]{1,0:T(8,128)(2,1)}), bf16[192,1664]{1,0:T(8,128)(2,1)}) %reduce-scatter.17.cloned.1.call-update) | async-done | bytes 638992 | tf_op jit(solution)/shard_map/reduce_scatter | solution.py:62
  576.1 31.0 %all-gather.18.cloned.1.call-done = bf16[512,1536]{1,0:T(8,128)(2,1)} async-done(((bf16[128,1536]{1,0:T(8,128)(2,1)}), bf16[512,1536]{1,0:T(8,128)(2,1)}) %all-gather.18.cloned.1.call-update) | async-done | bytes 1572880 | tf_op jit(solution)/shard_map/all_gather | solution.py:283
  607.1 3.5 convert_element_type.258
  610.7 31.6 %reduce-scatter.19.cloned.1.call-done = bf16[192,384]{1,0:T(8,128)(2,1)} async-done(((bf16[1536,384]{1,0:T(8,128)(2,1)}), bf16[192,384]{1,0:T(8,128)(2,1)}) %reduce-scatter.19.cloned.1.call-update) | async-done | bytes 147472 | tf_op jit(solution)/shard_map/reduce_scatter | solution.py:62
  642.3 14.6 %all_gather.36 = bf16[192,1536]{1,0:T(8,128)(2,1)S(1)} all-gather(bf16[192,384]{1,0:T(8,128)(2,1)} %reduce-scatter.19.cloned.1.call-done), channel_id=1, replica_groups=mesh['seq'=4,'wshard'=8] {'seq'}, dimensions={1}, use_global_device_ids=true | all-gather | bytes 737280 | tf_op jit(solution)/shard_map/all_gather | solution.py:76
  658.0 28.3 %all-gather.22.cloned.1.call-done = bf16[768,2048]{1,0:T(8,128)(2,1)} async-done(((bf16[192,2048]{1,0:T(8,128)(2,1)}), bf16[768,2048]{1,0:T(8,128)(2,1)}) %all-gather.22.cloned.1.call-update) | async-done | bytes 3145744 | tf_op jit(solution)/shard_map/all_gather | solution.py:284
  692.5 3.6 copy.88
  696.2 5.0 squeeze.16
  701.2 5.6 copy.87
  706.9 5.2 squeeze.15
  712.1 21.1 %reduce-scatter.15.cloned.1.call-done = bf16[256,1536]{1,0:T(8,128)(2,1)} async-done(((bf16[1024,1536]{1,0:T(8,128)(2,1)}), bf16[256,1536]{1,0:T(8,128)(2,1)}) %reduce-scatter.15.cloned.1.call-update) | async-done | bytes 786448 | tf_op jit(solution)/shard_map/reduce_scatter | solution.py:70
  735.0 40.3 %all-reduce.5 = (f32[1536]{0:T(1024)}, f32[24]{0:T(128)}, f32[1536]{0:T(1024)}) all-reduce(f32[1536]{0:T(1024)S(1)} %get-tuple-element.140, f32[24]{0:T(128)S(1)} %negate_dynamic-update-slice_fusion, f32[1536]{0:T(1024)S(1)} %get-tuple-element.138), channel_id=1, replica_groups=mesh['seq'=4,'wshard'=8] {'seq','wshard'}, use_global_device_ids=true, to_apply=%region_23.24 | all-reduce | flops 3096 | bytes 24768 | tf_op jit(solution)/shard_map/psum | solution.py:294
  775.4 5.4 reduce-scatter.11.cloned.1.call-done
  780.8 4.3 fusion.32
  785.0 36.4 %all-gather.20.cloned.1.call-done = bf16[768,1664]{1,0:T(8,128)(2,1)} async-done(((bf16[192,1664]{1,0:T(8,128)(2,1)}), bf16[768,1664]{1,0:T(8,128)(2,1)}) %all-gather.20.cloned.1.call-update) | async-done | bytes 2555920 | tf_op jit(solution)/shard_map/all_gather | solution.py:288
  (331 shorter events, 157.8 us)
Async XLA Ops:
  7.2 93.7 %all-gather.10.cloned.1.call-start = ((), (), s32[]{:S(2)}) async-start(), calls=%async_computation.10 | async-start | bytes 3932160 | tf_op jit(solution)/shard_map/all_gather | solution.py:66
  16.0 43.4 %collective-permute-start.1 = (bf16[192,1664]{1,0:T(8,128)(2,1)S(1)}, bf16[192,1664]{1,0:T(8,128)(2,1)S(1)}, u32[]{:S(2)}, u32[]{:S(2)}) collective-permute-start(bf16[192,1664]{1,0:T(8,128)(2,1)S(1)} %pad_dynamic-update-slice_fusion.1), channel_id=1, source_target_pairs={{0,7},{1,0},{2,1},{3,2},{4,3},{5,4},{6,5},{7,6},{8,15},{9,8},{10,9... | collective-permute-start | bytes 1916936 | tf_op jit(solution)/shard_map/ppermute | solution.py:26
  20.6 23.2 %collective-permute-start = (bf16[192,1664]{1,0:T(8,128)(2,1)S(1)}, bf16[192,1664]{1,0:T(8,128)(2,1)S(1)}, u32[]{:S(2)}, u32[]{:S(2)}) collective-permute-start(bf16[192,1664]{1,0:T(8,128)(2,1)S(1)} %pad_dynamic-update-slice_fusion.1), channel_id=1, source_target_pairs={{0,1},{1,2},{2,3},{3,4},{4,5},{5,6},{6,7},{7,0},{8,9},{9,10},{10,1... | collective-permute-start | bytes 1916936 | tf_op jit(solution)/shard_map/ppermute | solution.py:21
  23.3 16.2 %collective-permute-start.7 = (bf16[192,384]{1,0:T(8,128)(2,1)S(1)}, bf16[192,384]{1,0:T(8,128)(2,1)S(1)}, u32[]{:S(2)}, u32[]{:S(2)}) collective-permute-start(bf16[192,384]{1,0:T(8,128)(2,1)S(1)} %get-tuple-element.152), channel_id=1, source_target_pairs={{0,1},{1,2},{2,3},{3,4},{4,5},{5,6},{6,7},{7,0},{8,9},{9,10},{10,1... | collective-permute-start | bytes 442376 | tf_op jit(solution)/shard_map/ppermute | solution.py:21
  23.3 16.2 %collective-permute-start.8 = (bf16[192,384]{1,0:T(8,128)(2,1)S(1)}, bf16[192,384]{1,0:T(8,128)(2,1)S(1)}, u32[]{:S(2)}, u32[]{:S(2)}) collective-permute-start(bf16[192,384]{1,0:T(8,128)(2,1)S(1)} %get-tuple-element.152), channel_id=1, source_target_pairs={{0,7},{1,0},{2,1},{3,2},{4,3},{5,4},{6,5},{7,6},{8,15},{9,8},{10,9... | collective-permute-start | bytes 442376 | tf_op jit(solution)/shard_map/ppermute | solution.py:26
  32.7 71.3 %copy-start.42 = (f32[6]{0:T(128)}, f32[6]{0:T(128)S(1)}, u32[]{:S(2)}) copy-start(f32[6]{0:T(128)S(1)} %dynamic_slice.36) | copy-start | bytes 76
  39.6 7.9 collective-permute-start.9
  39.6 7.9 collective-permute-start.10
  43.8 27.3 %collective-permute-start.2 = (bf16[192,1664]{1,0:T(8,128)(2,1)S(1)}, bf16[192,1664]{1,0:T(8,128)(2,1)S(1)}, u32[]{:S(2)}, u32[]{:S(2)}) collective-permute-start(bf16[192,1664]{1,0:T(8,128)(2,1)S(1)} %collective-permute-done), channel_id=1, source_target_pairs={{0,1},{1,2},{2,3},{3,4},{4,5},{5,6},{6,7},{7,0},{8,9},{9,10},{10,1... | collective-permute-start | bytes 1916936 | tf_op jit(solution)/shard_map/ppermute | solution.py:21
  47.5 11.2 %collective-permute-start.11 = (bf16[192,384]{1,0:T(8,128)(2,1)S(1)}, bf16[192,384]{1,0:T(8,128)(2,1)S(1)}, u32[]{:S(2)}, u32[]{:S(2)}) collective-permute-start(bf16[192,384]{1,0:T(8,128)(2,1)S(1)} %collective-permute-done.9), channel_id=1, source_target_pairs={{0,1},{1,2},{2,3},{3,4},{4,5},{5,6},{6,7},{7,0},{8,9},{9,10},{10,1... | collective-permute-start | bytes 442376 | tf_op jit(solution)/shard_map/ppermute | solution.py:21
  47.5 15.4 %collective-permute-start.12 = (bf16[192,384]{1,0:T(8,128)(2,1)S(1)}, bf16[192,384]{1,0:T(8,128)(2,1)S(1)}, u32[]{:S(2)}, u32[]{:S(2)}) collective-permute-start(bf16[192,384]{1,0:T(8,128)(2,1)S(1)} %collective-permute-done.10), channel_id=1, source_target_pairs={{0,7},{1,0},{2,1},{3,2},{4,3},{5,4},{6,5},{7,6},{8,15},{9,8},{10,9... | collective-permute-start | bytes 442376 | tf_op jit(solution)/shard_map/ppermute | solution.py:26
  58.7 7.9 collective-permute-start.13
  59.4 17.0 %collective-permute-start.3 = (bf16[192,1664]{1,0:T(8,128)(2,1)S(1)}, bf16[192,1664]{1,0:T(8,128)(2,1)}, u32[]{:S(2)}, u32[]{:S(2)}) collective-permute-start(bf16[192,1664]{1,0:T(8,128)(2,1)S(1)} %collective-permute-done.1), channel_id=1, source_target_pairs={{0,7},{1,0},{2,1},{3,2},{4,3},{5,4},{6,5},{7,6},{8,15},{9,8},{10,9... | collective-permute-start | bytes 1916936 | tf_op jit(solution)/shard_map/ppermute | solution.py:26
  67.3 22.8 %all-to-all-start = ((bf16[4,384,384]{2,1,0:T(8,128)(2,1)}), bf16[4,384,384]{2,1,0:T(8,128)(2,1)S(1)}, u32[]{:S(2)}, u32[]{:S(2)}) async-start(bf16[4,384,384]{2,1,0:T(8,128)(2,1)} %bitcast.17), calls=%async_computation | async-start | bytes 2359296 | tf_op jit(solution)/shard_map/all_to_all | solution.py:212
  71.1 110.2 %reduce-scatter.9.cloned.1.call-start = ((), (), s32[]{:S(2)}) async-start(), calls=%async_computation.11 | async-start | bytes 3932160 | tf_op jit(solution)/shard_map/reduce_scatter | solution.py:70
  71.1 16.9 %collective-permute-start.4 = (bf16[192,1664]{1,0:T(8,128)(2,1)S(1)}, bf16[192,1664]{1,0:T(8,128)(2,1)}, u32[]{:S(2)}, u32[]{:S(2)}) collective-permute-start(bf16[192,1664]{1,0:T(8,128)(2,1)S(1)} %collective-permute-done.2), channel_id=1, source_target_pairs={{0,1},{1,2},{2,3},{3,4},{4,5},{5,6},{6,7},{7,0},{8,9},{9,10},{10,1... | collective-permute-start | bytes 1916936 | tf_op jit(solution)/shard_map/ppermute | solution.py:21
  76.4 18.6 %collective-permute-start.5 = (bf16[192,1664]{1,0:T(8,128)(2,1)}, bf16[192,1664]{1,0:T(8,128)(2,1)}, u32[]{:S(2)}, u32[]{:S(2)}) collective-permute-start(bf16[192,1664]{1,0:T(8,128)(2,1)} %collective-permute-done.3), channel_id=1, source_target_pairs={{0,7},{1,0},{2,1},{3,2},{4,3},{5,4},{6,5},{7,6},{8,15},{9,8},{10,9... | collective-permute-start | bytes 1916936 | tf_op jit(solution)/shard_map/ppermute | solution.py:26
  88.0 12.0 %collective-permute-start.6 = (bf16[192,1664]{1,0:T(8,128)(2,1)}, bf16[192,1664]{1,0:T(8,128)(2,1)S(1)}, u32[]{:S(2)}, u32[]{:S(2)}) collective-permute-start(bf16[192,1664]{1,0:T(8,128)(2,1)} %collective-permute-done.4), channel_id=1, source_target_pairs={{0,1},{1,2},{2,3},{3,4},{4,5},{5,6},{6,7},{7,0},{8,9},{9,10},{10,1... | collective-permute-start | bytes 1916936 | tf_op jit(solution)/shard_map/ppermute | solution.py:21
  90.9 43.3 %copy-start.14 = (bf16[384,4,384]{0,2,1:T(8,128)(2,1)}, bf16[384,4,384]{0,2,1:T(8,128)(2,1)S(1)}, u32[]{:S(2)}) copy-start(bf16[384,4,384]{0,2,1:T(8,128)(2,1)S(1)} %copy.75) | copy-start | bytes 3538948
  110.8 9.2 %copy-start.21 = (bf16[1024,384]{0,1:T(8,128)(2,1)}, bf16[1024,384]{0,1:T(8,128)(2,1)S(1)}, u32[]{:S(2)}) copy-start(bf16[1024,384]{0,1:T(8,128)(2,1)S(1)} %convolution_convert_fusion.8) | copy-start | bytes 2359300
  114.0 14.4 %copy-start.13 = (bf16[1024,384]{0,1:T(8,128)(2,1)}, bf16[1024,384]{0,1:T(8,128)(2,1)S(1)}, u32[]{:S(2)}) copy-start(bf16[1024,384]{0,1:T(8,128)(2,1)S(1)} %convolution_convert_fusion.10) | copy-start | bytes 2359300
  114.0 13.2 %copy-start.15 = (bf16[512,384]{0,1:T(8,128)(2,1)}, bf16[512,384]{0,1:T(8,128)(2,1)S(1)}, u32[]{:S(2)}) copy-start(bf16[512,384]{0,1:T(8,128)(2,1)S(1)} %slice.294) | copy-start | bytes 1179652
  119.0 8.2 copy-start.3
  138.9 136.1 %all-gather.14.cloned.1.call-start = ((), (), s32[]{:S(2)}) async-start(), calls=%async_computation.14 | async-start | bytes 3932160 | tf_op jit(solution)/shard_map/all_gather | solution.py:66
  141.1 142.2 %all-gather.12.cloned.1.call-start = ((), (), s32[]{:S(2)}) async-start(), calls=%async_computation.12 | async-start | bytes 3932160 | tf_op jit(solution)/shard_map/all_gather | solution.py:66
  143.7 37.5 %copy-start.4 = (bf16[1,256,1536]{2,1,0:T(8,128)(2,1)S(1)}, bf16[1,256,1536]{2,1,0:T(8,128)(2,1)}, u32[]{:S(2)}) copy-start(bf16[1,256,1536]{2,1,0:T(8,128)(2,1)} %param.37) | copy-start | bytes 2359300
  147.6 35.1 %copy-start.36 = (f32[1536]{0:T(1024)S(1)}, f32[1536]{0:T(1024)}, u32[]{:S(2)}) copy-start(f32[1536]{0:T(1024)} %param.47) | copy-start | bytes 18436
  154.4 50.5 %collective-permute-start.14 = (bf16[192,2048]{1,0:T(8,128)(2,1)S(1)}, bf16[192,2048]{1,0:T(8,128)(2,1)}, u32[]{:S(2)}, u32[]{:S(2)}) collective-permute-start(bf16[192,2048]{1,0:T(8,128)(2,1)S(1)} %bitcast_dynamic-update-slice_fusion), channel_id=1, source_target_pairs={{0,1},{1,2},{2,3},{3,4},{4,5},{5,6},{6,7},{7,0},{8,9},{9,10},{10,1... | collective-permute-start | bytes 2359304 | tf_op jit(solution)/shard_map/ppermute | solution.py:21
  185.1 168.3 %reduce-scatter.13.cloned.1.call-start = ((), (), s32[]{:S(2)}) async-start(), calls=%async_computation.15 | async-start | bytes 3932160 | tf_op jit(solution)/shard_map/reduce_scatter | solution.py:70
  188.9 11.6 %collective-permute-start.21 = (bf16[128,1536]{1,0:T(8,128)(2,1)}, bf16[128,1536]{1,0:T(8,128)(2,1)S(1)}, u32[]{:S(2)}, u32[]{:S(2)}) collective-permute-start(bf16[128,1536]{1,0:T(8,128)(2,1)} %get-tuple-element.150), channel_id=1, source_target_pairs={{0,1},{1,2},{2,3},{3,4},{4,5},{5,6},{6,7},{7,0},{8,9},{9,10},{10,1... | collective-permute-start | bytes 1179656 | tf_op jit(solution)/shard_map/ppermute | solution.py:21
  188.9 11.6 %collective-permute-start.22 = (bf16[128,1536]{1,0:T(8,128)(2,1)}, bf16[128,1536]{1,0:T(8,128)(2,1)S(1)}, u32[]{:S(2)}, u32[]{:S(2)}) collective-permute-start(bf16[128,1536]{1,0:T(8,128)(2,1)} %get-tuple-element.150), channel_id=1, source_target_pairs={{0,7},{1,0},{2,1},{3,2},{4,3},{5,4},{6,5},{7,6},{8,15},{9,8},{10,9... | collective-permute-start | bytes 1179656 | tf_op jit(solution)/shard_map/ppermute | solution.py:26
  192.5 23.6 %collective-permute-start.15 = (bf16[192,2048]{1,0:T(8,128)(2,1)S(1)}, bf16[192,2048]{1,0:T(8,128)(2,1)}, u32[]{:S(2)}, u32[]{:S(2)}) collective-permute-start(bf16[192,2048]{1,0:T(8,128)(2,1)S(1)} %bitcast_dynamic-update-slice_fusion), channel_id=1, source_target_pairs={{0,7},{1,0},{2,1},{3,2},{4,3},{5,4},{6,5},{7,6},{8,15},{9,8},{10,9... | collective-permute-start | bytes 2359304 | tf_op jit(solution)/shard_map/ppermute | solution.py:26
  200.5 19.4 %collective-permute-start.23 = (bf16[128,1536]{1,0:T(8,128)(2,1)S(1)}, bf16[128,1536]{1,0:T(8,128)(2,1)S(1)}, u32[]{:S(2)}, u32[]{:S(2)}) collective-permute-start(bf16[128,1536]{1,0:T(8,128)(2,1)S(1)} %collective-permute-done.21), channel_id=1, source_target_pairs={{0,1},{1,2},{2,3},{3,4},{4,5},{5,6},{6,7},{7,0},{8,9},{9,10},{10,1... | collective-permute-start | bytes 1179656 | tf_op jit(solution)/shard_map/ppermute | solution.py:21
  200.5 24.0 %collective-permute-start.24 = (bf16[128,1536]{1,0:T(8,128)(2,1)S(1)}, bf16[128,1536]{1,0:T(8,128)(2,1)S(1)}, u32[]{:S(2)}, u32[]{:S(2)}) collective-permute-start(bf16[128,1536]{1,0:T(8,128)(2,1)S(1)} %collective-permute-done.22), channel_id=1, source_target_pairs={{0,7},{1,0},{2,1},{3,2},{4,3},{5,4},{6,5},{7,6},{8,15},{9,8},{10,9... | collective-permute-start | bytes 1179656 | tf_op jit(solution)/shard_map/ppermute | solution.py:26
  204.8 28.4 %collective-permute-start.16 = (bf16[192,2048]{1,0:T(8,128)(2,1)}, bf16[192,2048]{1,0:T(8,128)(2,1)S(1)}, u32[]{:S(2)}, u32[]{:S(2)}) collective-permute-start(bf16[192,2048]{1,0:T(8,128)(2,1)} %collective-permute-done.14), channel_id=1, source_target_pairs={{0,1},{1,2},{2,3},{3,4},{4,5},{5,6},{6,7},{7,0},{8,9},{9,10},{10,1... | collective-permute-start | bytes 2359304 | tf_op jit(solution)/shard_map/ppermute | solution.py:21
  216.1 34.5 %collective-permute-start.17 = (bf16[192,2048]{1,0:T(8,128)(2,1)}, bf16[192,2048]{1,0:T(8,128)(2,1)S(1)}, u32[]{:S(2)}, u32[]{:S(2)}) collective-permute-start(bf16[192,2048]{1,0:T(8,128)(2,1)} %collective-permute-done.15), channel_id=1, source_target_pairs={{0,7},{1,0},{2,1},{3,2},{4,3},{5,4},{6,5},{7,6},{8,15},{9,8},{10,9... | collective-permute-start | bytes 2359304 | tf_op jit(solution)/shard_map/ppermute | solution.py:26
  219.9 19.1 %collective-permute-start.25 = (bf16[128,1536]{1,0:T(8,128)(2,1)S(1)}, bf16[128,1536]{1,0:T(8,128)(2,1)S(1)}, u32[]{:S(2)}, u32[]{:S(2)}) collective-permute-start(bf16[128,1536]{1,0:T(8,128)(2,1)S(1)} %collective-permute-done.23), channel_id=1, source_target_pairs={{0,1},{1,2},{2,3},{3,4},{4,5},{5,6},{6,7},{7,0},{8,9},{9,10},{10,1... | collective-permute-start | bytes 1179656 | tf_op jit(solution)/shard_map/ppermute | solution.py:21
  224.5 25.3 %collective-permute-start.26 = (bf16[128,1536]{1,0:T(8,128)(2,1)S(1)}, bf16[128,1536]{1,0:T(8,128)(2,1)S(1)}, u32[]{:S(2)}, u32[]{:S(2)}) collective-permute-start(bf16[128,1536]{1,0:T(8,128)(2,1)S(1)} %collective-permute-done.24), channel_id=1, source_target_pairs={{0,7},{1,0},{2,1},{3,2},{4,3},{5,4},{6,5},{7,6},{8,15},{9,8},{10,9... | collective-permute-start | bytes 1179656 | tf_op jit(solution)/shard_map/ppermute | solution.py:26
  233.2 22.1 %collective-permute-start.18 = (bf16[192,2048]{1,0:T(8,128)(2,1)S(1)}, bf16[192,2048]{1,0:T(8,128)(2,1)S(1)}, u32[]{:S(2)}, u32[]{:S(2)}) collective-permute-start(bf16[192,2048]{1,0:T(8,128)(2,1)S(1)} %collective-permute-done.16), channel_id=1, source_target_pairs={{0,1},{1,2},{2,3},{3,4},{4,5},{5,6},{6,7},{7,0},{8,9},{9,10},{10,1... | collective-permute-start | bytes 2359304 | tf_op jit(solution)/shard_map/ppermute | solution.py:21
  239.0 21.1 %collective-permute-start.27 = (bf16[128,1536]{1,0:T(8,128)(2,1)S(1)}, bf16[128,1536]{1,0:T(8,128)(2,1)S(1)}, u32[]{:S(2)}, u32[]{:S(2)}) collective-permute-start(bf16[128,1536]{1,0:T(8,128)(2,1)S(1)} %collective-permute-done.25), channel_id=1, source_target_pairs={{0,1},{1,2},{2,3},{3,4},{4,5},{5,6},{6,7},{7,0},{8,9},{9,10},{10,1... | collective-permute-start | bytes 1179656 | tf_op jit(solution)/shard_map/ppermute | solution.py:21
  250.5 20.7 %collective-permute-start.19 = (bf16[192,2048]{1,0:T(8,128)(2,1)S(1)}, bf16[192,2048]{1,0:T(8,128)(2,1)S(1)}, u32[]{:S(2)}, u32[]{:S(2)}) collective-permute-start(bf16[192,2048]{1,0:T(8,128)(2,1)S(1)} %collective-permute-done.17), channel_id=1, source_target_pairs={{0,7},{1,0},{2,1},{3,2},{4,3},{5,4},{6,5},{7,6},{8,15},{9,8},{10,9... | collective-permute-start | bytes 2359304 | tf_op jit(solution)/shard_map/ppermute | solution.py:26
  255.3 18.7 %collective-permute-start.20 = (bf16[192,2048]{1,0:T(8,128)(2,1)S(1)}, bf16[192,2048]{1,0:T(8,128)(2,1)S(1)}, u32[]{:S(2)}, u32[]{:S(2)}) collective-permute-start(bf16[192,2048]{1,0:T(8,128)(2,1)S(1)} %collective-permute-done.18), channel_id=1, source_target_pairs={{0,1},{1,2},{2,3},{3,4},{4,5},{5,6},{6,7},{7,0},{8,9},{9,10},{10,1... | collective-permute-start | bytes 2359304 | tf_op jit(solution)/shard_map/ppermute | solution.py:21
  310.6 42.8 %copy-start.6 = (bf16[256,1536]{1,0:T(8,128)(2,1)S(1)}, bf16[256,1536]{1,0:T(8,128)(2,1)}, u32[]{:S(2)}) copy-start(bf16[256,1536]{1,0:T(8,128)(2,1)} %reduce-scatter.9.cloned.1.call-done) | copy-start | bytes 2359300
  310.7 91.4 %all-gather.16.cloned.1.call-start = ((), (), s32[]{:S(2)}) async-start(), calls=%async_computation.16 | async-start | bytes 3932160 | tf_op jit(solution)/shard_map/all_gather | solution.py:66
  358.0 99.9 %reduce-scatter.23.cloned.1.call-start = ((), (), s32[]{:S(2)}) async-start(), calls=%async_computation.21 | async-start | bytes 3538944 | tf_op jit(solution)/shard_map/reduce_scatter | solution.py:62
  365.7 150.9 %reduce-scatter.21.cloned.1.call-start = ((), (), s32[]{:S(2)}) async-start(), calls=%async_computation.20 | async-start | bytes 7077888 | tf_op jit(solution)/shard_map/reduce_scatter | solution.py:62
  378.8 34.6 %slice-start.6 = ((s8[6291456]{0:T(1024)(128)(4,1)}), s8[2097152]{0:T(1024)(128)(4,1)S(1)}, s32[]{:S(2)}) async-start(s8[6291456]{0:T(1024)(128)(4,1)} %bitcast.204), calls=%async_computation.31 | async-start | bytes 4194304
  378.8 197.3 %reduce-scatter.17.cloned.1.call-start = ((), (), s32[]{:S(2)}) async-start(), calls=%async_computation.18 | async-start | bytes 5750784 | tf_op jit(solution)/shard_map/reduce_scatter | solution.py:62
  408.2 8.5 %slice-start = ((s8[12582912]{0:T(1024)(128)(4,1)}), s8[4194304]{0:T(1024)(128)(4,1)S(1)}, s32[]{:S(2)}) async-start(s8[12582912]{0:T(1024)(128)(4,1)} %bitcast.200), calls=%async_computation.25 | async-start | bytes 8388608
  408.2 8.5 %slice-start.1 = ((s8[12582912]{0:T(1024)(128)(4,1)}), s8[4194304]{0:T(1024)(128)(4,1)S(1)}, s32[]{:S(2)}) async-start(s8[12582912]{0:T(1024)(128)(4,1)} %bitcast.200), calls=%async_computation.26 | async-start | bytes 8388608
  421.0 8.7 %copy-start.29 = (bf16[512,384]{0,1:T(8,128)(2,1)S(1)}, bf16[512,384]{0,1:T(8,128)(2,1)}, u32[]{:S(2)}) copy-start(bf16[512,384]{0,1:T(8,128)(2,1)} %copy-done.28) | copy-start | bytes 1179652
  429.7 9.1 %slice-start.10 = ((s8[6291456]{0:T(1024)(128)(4,1)}), s8[4194304]{0:T(1024)(128)(4,1)S(1)}, s32[]{:S(2)}) async-start(s8[6291456]{0:T(1024)(128)(4,1)} %bitcast.208), calls=%async_computation.35 | async-start | bytes 8388608
  432.5 7.7 slice-start.8
  457.8 149.3 %all-gather.18.cloned.1.call-start = ((), (), s32[]{:S(2)}) async-start(), calls=%async_computation.22 | async-start | bytes 1966080 | tf_op jit(solution)/shard_map/all_gather | solution.py:283
  458.4 183.9 %reduce-scatter.19.cloned.1.call-start = ((), (), s32[]{:S(2)}) async-start(), calls=%async_computation.19 | async-start | bytes 1327104 | tf_op jit(solution)/shard_map/reduce_scatter | solution.py:62
  480.8 205.5 %all-gather.22.cloned.1.call-start = ((), (), s32[]{:S(2)}) async-start(), calls=%async_computation.24 | async-start | bytes 3932160 | tf_op jit(solution)/shard_map/all_gather | solution.py:284
  516.7 216.5 %reduce-scatter.15.cloned.1.call-start = ((), (), s32[]{:S(2)}) async-start(), calls=%async_computation.17 | async-start | bytes 3932160 | tf_op jit(solution)/shard_map/reduce_scatter | solution.py:70
  526.9 253.9 %reduce-scatter.11.cloned.1.call-start = ((), (), s32[]{:S(2)}) async-start(), calls=%async_computation.13 | async-start | bytes 3932160 | tf_op jit(solution)/shard_map/reduce_scatter | solution.py:70
  535.2 286.2 %all-gather.20.cloned.1.call-start = ((), (), s32[]{:S(2)}) async-start(), calls=%async_computation.23 | async-start | bytes 3194880 | tf_op jit(solution)/shard_map/all_gather | solution.py:288
  706.9 26.3 %copy-start.37 = (f32[1536]{0:T(1024)S(1)}, f32[1536]{0:T(1024)}, u32[]{:S(2)}) copy-start(f32[1536]{0:T(1024)} %param.39) | copy-start | bytes 18436
  706.9 26.3 %copy-start.39 = (f32[256]{0:T(256)S(1)}, f32[256]{0:T(256)}, u32[]{:S(2)}) copy-start(f32[256]{0:T(256)} %copy-done.38) | copy-start | bytes 3076
  706.9 68.5 %copy-start.41 = (f32[256]{0:T(256)S(1)}, f32[256]{0:T(256)}, u32[]{:S(2)}) copy-start(f32[256]{0:T(256)} %copy-done.40) | copy-start | bytes 3076
  706.9 73.9 %copy-start.7 = (bf16[256,1536]{1,0:T(8,128)(2,1)S(1)}, bf16[256,1536]{1,0:T(8,128)(2,1)}, u32[]{:S(2)}) copy-start(bf16[256,1536]{1,0:T(8,128)(2,1)} %reduce-scatter.9.cloned.1.call-done) | copy-start | bytes 2359300
  706.9 73.9 %copy-start.9 = (bf16[1,256,1536]{2,1,0:T(8,128)(2,1)S(1)}, bf16[1,256,1536]{2,1,0:T(8,128)(2,1)}, u32[]{:S(2)}) copy-start(bf16[1,256,1536]{2,1,0:T(8,128)(2,1)} %param.51) | copy-start | bytes 2359300
  (43 other events, 143.4 us)
Sparse Core Ops, SparseCore 0:
  12.2 46.5 all-gather.9
  139.0 42.1 reduce-scatter.8
  183.6 43.8 all-gather.13
  229.8 43.8 all-gather.11
  310.8 42.5 reduce-scatter.12
  358.1 43.8 all-gather.15
  404.9 40.3 reduce-scatter.22
  447.6 68.9 reduce-scatter.20
  519.0 57.0 reduce-scatter.16
  577.7 29.3 all-gather.17
  609.4 32.8 reduce-scatter.18
  644.0 42.2 all-gather.21
  689.3 43.8 reduce-scatter.14
  736.0 44.6 reduce-scatter.10
  782.5 38.9 all-gather.19
